TPU v7x, 32 devices: a whole 2x2x4 slice. The times are simulated.
32 devices in a mesh: rep: 8 (over y, x, core), tp: 4 (over z).
Axes of the slice: x: 2, y: 2, z: 4, core: 2. Of those that a mesh axis runs over, the one named last changes fastest.
Arguments:
- hidden: bfloat16 [512, 8192], P('rep'), may hold values from -6 to 6
- norm_gain: bfloat16 [8192], replicated, may hold values from 0.5 to 1.5
- query_weight_matrix: bfloat16 [8192, 4096], P(None, 'tp'), may hold values from -0.0625 to 0.0625
- key_value_weight: bfloat16 [2, 8192, 1024], P(None, None, 'tp'), may hold values from -0.0625 to 0.0625
- output_weight_matrix: bfloat16 [4096, 8192], P('tp'), may hold values from -0.375 to 0.375
- input_down_factors: bfloat16 [3, 8192, 64], P(None, ('rep', 'tp')), may hold values from -0.0625 to 0.0625
- query_up_factor: bfloat16 [64, 4096], P(None, ('rep', 'tp')), may hold values from -0.75 to 0.75
- key_value_up_factors: bfloat16 [2, 64, 1024], P(None, None, ('rep', 'tp')), may hold values from -0.75 to 0.75
- output_down_factor: bfloat16 [4096, 64], P(('rep', 'tp')), may hold values from -0.375 to 0.375
- output_up_factor: bfloat16 [64, 8192], P(None, ('rep', 'tp')), may hold values from -0.75 to 0.75
- cache_keys: bfloat16 [512, 8, 128, 128], P('rep', 'tp'), may hold values from -360 to 360
- cache_values: bfloat16 [512, 8, 128, 128], P('rep', 'tp'), may hold values from -6 to 6
- lengths: int32 [512], P('rep'), may hold values from 1 to 127
Outputs:
- attn_out: bfloat16 [512, 8192], P('rep', 'tp')
All inputs are finite; a program needn't handle non-finite values.
Results may differ from a plain program's by a relative error of at most 0.03.
Values may be sent and summed in bfloat16 or wider, within the bound.
A program may use at most 128 MiB of HBM per device.

v0:
```python
import functools
import math

import jax
import jax.numpy as jnp
from jax import lax
from jax.experimental import pallas as pl
from jax.experimental.pallas import tpu as pltpu
from jax.sharding import PartitionSpec as P

epsilon = 1e-06
rope_base = 1000000.0
adapter_scale = 0.5

f32 = jnp.float32
bf16 = jnp.bfloat16
LANES = 128
MESH_ID = pl.DeviceIdType.MESH


def nt_dot(left, right):
    return lax.dot_general(
        left, right, (((1,), (1,)), ((), ())), preferred_element_type=f32
    )


def nn_dot(left, right):
    return jnp.dot(left, right, preferred_element_type=f32)


def channels_of(n):
    return ((1, 0, n // 2), (-1, 1, n // 2), (1, 1, n // 2 - 1), (-1, 0, n // 2 - 1))


def kernel(
    dims,
    hidden,
    gain,
    wq,
    wkv,
    wo,
    dn_own,
    f_q,
    f_kv,
    f_od,
    f_ou,
    cache_k,
    cache_v,
    lengths,
    out,
    hid_b,
    norm_b,
    wq_b,
    wkv_b,
    wo_b,
    k_b,
    v_b,
    dn_b,
    a_q,
    a_kv,
    a_od,
    a_ou,
    g_q,
    g_kv,
    g_od,
    g_ou,
    angle,
    q_acc,
    kv_acc,
    inner_o,
    inner_s,
    inner_r,
    q3,
    nk3,
    nv3,
    c3,
    ctx,
    mid_s,
    mid_r,
    rs_s,
    rs_r,
    hid_sem,
    w_sem,
    kv_sem,
    wo_sem,
    k_sem,
    v_sem,
    own_sem,
    dn_ssem,
    dn_rsem,
    dn_fsem,
    a_ssem,
    a_rsem,
    g_ssem,
    g_rsem,
    g_fsem,
    in_ssem,
    in_rsem,
    mid_ssem,
    mid_rsem,
    rs_ssem,
    rs_rsem,
):
    n, reps = dims["tp"], dims["rep"]
    seqs, depth = hidden.shape
    head_dim = cache_k.shape[3]
    kv_local = cache_k.shape[1]
    heads = wq.shape[1] // head_dim
    group = heads // kv_local
    pad_heads = q3.shape[0] // seqs
    rank = dims["rank"]
    block, win = dims["block"], dims["win"]
    half_reps = reps // 2
    r = lax.axis_index("rep")
    t = lax.axis_index("tp")
    core = lax.rem(r, 2)
    partner = r + 1 - 2 * core

    own_dn = pltpu.make_async_copy(dn_own, dn_b.at[r], own_sem.at[0])
    mine_at = r // 2
    spread = (a_q, a_kv, a_od, a_ou)
    gathered = (g_q, g_kv, g_od, g_ou)
    own_f = [
        pltpu.make_async_copy(src, dst.at[mine_at], own_sem.at[1 + f])
        for f, (src, dst) in enumerate(zip((f_q, f_kv, f_od, f_ou), spread))
    ]
    own_dn.start()
    for c in own_f:
        c.start()
    hid = pltpu.make_async_copy(hidden, hid_b, hid_sem)
    hid.start()
    steps = w_sem.shape[0]
    kc = depth // steps

    def w_copies(i):
        rows = pl.ds(pl.multiple_of(i * kc, kc), kc)
        return (
            pltpu.make_async_copy(wq.at[rows, :], wq_b.at[rows, :], w_sem.at[i]),
            pltpu.make_async_copy(wkv.at[:, rows, :], wkv_b.at[:, rows, :], kv_sem.at[i]),
        )

    @pl.loop(0, steps)
    def _(i):
        for c in w_copies(i):
            c.start()

    parts = k_sem.shape[0]
    ps = seqs // parts

    def cache_copies(i):
        rows = pl.ds(i * ps, ps)
        return (
            pltpu.make_async_copy(cache_k.at[rows], k_b.at[rows], k_sem.at[i]),
            pltpu.make_async_copy(cache_v.at[rows], v_b.at[rows], v_sem.at[i]),
        )

    @pl.loop(0, parts)
    def _(i):
        for c in cache_copies(i):
            c.start()

    wide = wo.shape[1] // n
    half_w = wide // 2

    def out_cols(k, half):
        d = lax.rem(t + k + n, n)
        return pl.ds(pl.multiple_of(d * wide + half * half_w, LANES), half_w)

    def wo_copy(k, half):
        cols = out_cols(k, half)
        idx = (k % n) * 2 + half
        return pltpu.make_async_copy(wo.at[:, cols], wo_b.at[idx], wo_sem.at[idx])

    sends = []
    for k in range(n // 2, 0, -1):
        for fresh in (True, False):
            for ci, (way, half, hops) in enumerate(channels_of(n)):
                if k <= hops and (k == hops) == fresh:
                    sends.append((ci, way, half, hops, k))
    for _ci, way, half, _hops, k in sends:
        wo_copy(way * k, half).start()
    wo_copy(0, 0).start()
    wo_copy(0, 1).start()

    barrier = pltpu.get_barrier_semaphore()

    def greet(rr, tt):
        pl.semaphore_signal(barrier, inc=1, device_id=(rr, tt), device_id_type=MESH_ID)

    count = 0
    greet(partner, t)
    count += 1
    for j in range(1, n):
        greet(r, lax.rem(t + j, n))
        count += 1
    for j in range(1, half_reps):
        greet(lax.rem(r + 2 * j, reps), t)
        count += 1

    pl.semaphore_wait(barrier, count)

    def remote(src, dst, ssem, rsem, rr, tt):
        return pltpu.make_async_remote_copy(
            src_ref=src,
            dst_ref=dst,
            send_sem=ssem,
            recv_sem=rsem,
            device_id=(rr, tt),
            device_id_type=MESH_ID,
        )

    own_dn.wait()
    dn_sends = []
    for j in range(1, half_reps):
        dn_sends.append(
            remote(
                dn_b.at[r], dn_b.at[r], dn_ssem.at[j], dn_rsem.at[r],
                lax.rem(r + 2 * j, reps), t,
            )
        )
    dn_sends.append(
        remote(dn_b.at[r], dn_b.at[r], dn_fsem.at[0], dn_rsem.at[r], partner, t)
    )
    for c in dn_sends:
        c.start()
    a_sends = []

    def to_chips(f):
        buf = spread[f]
        own_f[f].wait()
        for j in range(1, half_reps):
            c = remote(
                buf.at[mine_at], buf.at[mine_at], a_ssem.at[f, j], a_rsem.at[f, mine_at],
                lax.rem(r + 2 * j, reps), t,
            )
            c.start()
            a_sends.append(c)

    to_chips(0)
    to_chips(1)
    per_plane = reps // n
    groups = per_plane // 2
    g_sends = []

    def to_planes(f):
        buf, full = spread[f], gathered[f]
        for j in range(1, half_reps):
            src = lax.rem(r + 2 * j, reps) // 2
            remote(
                buf.at[src], buf.at[src], a_ssem.at[f, j], a_rsem.at[f, src], r, t
            ).wait_recv()
        for i in range(groups):
            s = n * (2 * i + core) + t
            for j in range(1, n):
                plane = lax.rem(t + j, n)
                src = (plane * per_plane + 2 * i) // 2
                c = remote(
                    buf.at[src], full.at[s], g_ssem.at[f, i * n + j], g_rsem.at[f, s],
                    r, plane,
                )
                c.start()
                g_sends.append(c)
            src = (t * per_plane + 2 * i) // 2
            pltpu.make_async_copy(buf.at[src], full.at[s], g_rsem.at[f, s]).start()

    def across(f):
        full = gathered[f]
        for i in range(groups):
            for z in range(n):
                s = n * (2 * i + core) + z
                pltpu.make_async_copy(spread[f].at[0], full.at[s], g_rsem.at[f, s]).wait()
                c = remote(
                    full.at[s], full.at[s], g_fsem.at[f, i * n + z], g_rsem.at[f, s],
                    partner, t,
                )
                c.start()
                g_sends.append(c)

    def settled(f):
        full = gathered[f]
        for i in range(groups):
            for z in range(n):
                s = n * (2 * i + 1 - core) + z
                pltpu.make_async_copy(spread[f].at[0], full.at[s], g_rsem.at[f, s]).wait()

    half_dim = head_dim // 2
    step = lax.rem(lax.broadcasted_iota(jnp.int32, (1, head_dim), 1), half_dim)
    frequency = jnp.exp(step.astype(f32) * (-2.0 * math.log(rope_base) / head_dim))

    @pl.loop(0, seqs // 8)
    def _(i):
        for b in range(8):
            angle[pl.ds(i * 8 + b, 1), :] = lengths[i * 8 + b].astype(f32) * frequency

    hid.wait()

    @pl.loop(0, seqs // 16)
    def _(i):
        rows = pl.ds(pl.multiple_of(i * 16, 16), 16)
        x = hid_b[rows, :].astype(f32)
        square = jnp.mean(x * x, axis=-1, keepdims=True)
        norm_b[rows, :] = (
            x * lax.rsqrt(square + epsilon) * gain[...].astype(f32).reshape(1, depth)
        ).astype(bf16)

    q_acc[...] = jnp.zeros_like(q_acc)
    kv_acc[...] = jnp.zeros_like(kv_acc)

    def project(lo, hi):
        @pl.loop(lo, hi)
        def _(i):
            for c in w_copies(i):
                c.wait()
            rows = pl.ds(pl.multiple_of(i * kc, kc), kc)
            x = norm_b[:, rows]
            q_acc[...] += nn_dot(x, wq_b[rows, :])
            for j in range(2):
                kv_acc[j] += nn_dot(x, wkv_b[j, rows, :])

    project(0, steps // 4)
    dn_fwd = []
    for j in range(half_reps - 1, 0, -1):
        src = lax.rem(r + 2 * j, reps)
        remote(dn_b.at[src], dn_b.at[src], dn_fsem.at[j], dn_rsem.at[src], partner, t).wait_recv()
        c = remote(dn_b.at[src], dn_b.at[src], dn_fsem.at[j], dn_rsem.at[src], partner, t)
        c.start()
        dn_fwd.append(c)
    to_planes(0)
    to_planes(1)
    project(steps // 4, steps // 2)

    for j in range(half_reps):
        src = lax.rem(partner + 2 * j, reps)
        remote(dn_b.at[src], dn_b.at[src], dn_fsem.at[j], dn_rsem.at[src], partner, t).wait_recv()

    part = jnp.zeros((seqs, 3 * rank), f32)
    for j in range(reps):
        start = (j * n + t) * block
        cols = pl.ds(pl.multiple_of(start // win * win, LANES), win)
        part = part + nt_dot(norm_b[:, cols], dn_b[j])
    inner_s[...] = part.astype(bf16)
    inner_o[...] = part
    in_sends = []
    for j in range(1, n):
        c = remote(
            inner_s, inner_r.at[j], in_ssem.at[j], in_rsem.at[j], r, lax.rem(t + j, n)
        )
        c.start()
        in_sends.append(c)

    across(0)
    across(1)
    to_chips(2)
    to_chips(3)
    project(steps // 2, 3 * steps // 4)
    to_planes(2)
    to_planes(3)
    project(3 * steps // 4, steps)
    settled(0)
    settled(1)

    total = inner_o[...]
    for c in in_sends:
        c.wait_recv()
    for j in range(1, n):
        total = total + inner_r[j].astype(f32)
    inner = total.astype(bf16).astype(f32)
    inner_q = inner[:, :rank].astype(bf16)
    inner_k = inner[:, rank : 2 * rank].astype(bf16)
    inner_v = inner[:, 2 * rank :].astype(bf16)

    def rows_of(j):
        w = g_kv.shape[2]
        return g_kv[:, j].astype(f32).reshape(reps * w, rank).astype(bf16)

    q_up = jnp.concatenate([g_q[s] for s in range(reps)], axis=1)
    q = q_acc[...] + adapter_scale * nn_dot(inner_q, q_up)
    nk = kv_acc[0] + adapter_scale * nt_dot(inner_k, rows_of(0))
    nv = kv_acc[1] + adapter_scale * nt_dot(inner_v, rows_of(1))

    across(2)
    across(3)

    cosv = jnp.cos(angle[...])
    sinv = jnp.sin(angle[...])
    lane = lax.broadcasted_iota(jnp.int32, (seqs, head_dim), 1)
    sinv = jnp.where(lane < half_dim, -sinv, sinv)

    def turn(x):
        return x * cosv + pltpu.roll(x, head_dim // 2, 1) * sinv

    for h in range(pad_heads):
        rows = pl.ds(h, seqs, stride=pad_heads)
        if h < heads:
            q3[rows, :] = turn(q[:, h * head_dim : (h + 1) * head_dim])
        else:
            q3[rows, :] = jnp.zeros((seqs, head_dim), f32)
    for j in range(kv_local):
        key = turn(nk[:, j * head_dim : (j + 1) * head_dim]).astype(bf16).astype(f32)
        val = nv[:, j * head_dim : (j + 1) * head_dim].astype(bf16).astype(f32)
        for g in range(pad_heads):
            if min(g // group, kv_local - 1) == j:
                rows = pl.ds(g, seqs, stride=pad_heads)
                nk3[rows, :] = key
                nv3[rows, :] = val

    cache = cache_k.shape[2]
    span = kv_local * cache
    score_scale = 1.0 / math.sqrt(head_dim)
    bs = min(16, ps)
    per = ps // bs

    def attend(i):
        @pl.when(lax.rem(i, per) == 0)
        def _():
            for c in cache_copies(i // per):
                c.wait()

        base = pl.multiple_of(i * (bs * pad_heads), bs * pad_heads)
        rows = pl.ds(base, bs * pad_heads)
        qq = q3[rows, :]
        hi = qq.astype(bf16).astype(f32)
        rest = qq - hi
        mid = rest.astype(bf16).astype(f32)
        low = rest - mid
        own = jnp.sum(qq * nk3[rows, :], axis=-1, keepdims=True) * score_scale
        row_id = lax.broadcasted_iota(jnp.int32, (pad_heads, span), 0)
        col_id = lax.broadcasted_iota(jnp.int32, (pad_heads, span), 1)
        mine = jnp.minimum(row_id // group, kv_local - 1) == col_id // cache
        pos = lax.rem(col_id, cache)
        scored = []
        for b in range(bs):
            sl = slice(b * pad_heads, (b + 1) * pad_heads)
            stack = jnp.concatenate([hi[sl], mid[sl], low[sl]], axis=0).astype(bf16)
            keys = k_b[i * bs + b].reshape(span, head_dim)
            dots = nt_dot(stack, keys)
            sc = (
                dots[:pad_heads]
                + dots[pad_heads : 2 * pad_heads]
                + dots[2 * pad_heads :]
            ) * score_scale
            live = jnp.logical_and(mine, pos < lengths[i * bs + b])
            scored.append(jnp.where(live, sc, -1e30))
        sc = jnp.concatenate(scored, axis=0)
        top = jnp.maximum(jnp.max(sc, axis=-1, keepdims=True), own)
        w = jnp.exp(sc - top)
        ow = jnp.exp(own - top)
        scale = 1.0 / (jnp.sum(w, axis=-1, keepdims=True) + ow)
        probs = w * scale
        own_part = (ow * scale).astype(bf16).astype(f32) * nv3[rows, :]
        for b in range(bs):
            sl = slice(b * pad_heads, (b + 1) * pad_heads)
            vals = v_b[i * bs + b].reshape(span, head_dim)
            here = pl.ds(base + b * pad_heads, pad_heads)
            c3[here, :] = nn_dot(probs[sl].astype(bf16), vals) + own_part[sl]

    waves = rs_s.shape[0]
    ws = seqs // waves

    def attend_wave(wave):
        pl.loop(wave * ws // bs, (wave + 1) * ws // bs)(attend)
        for h in range(heads):
            ctx[wave * ws : (wave + 1) * ws, h * head_dim : (h + 1) * head_dim] = c3[
                pl.ds(wave * ws * pad_heads + h, ws, stride=pad_heads), :
            ].astype(bf16)

    tile = min(512, half_w)
    offsets = []
    at = 0
    for _way, _half, hops in channels_of(n):
        offsets.append(at)
        at += hops
    rs_sends = []

    def hop(wave, place, way):
        return remote(
            rs_s.at[wave, place], rs_r.at[wave, place], rs_ssem.at[wave, place],
            rs_rsem.at[wave, place], r, lax.rem(t + way + n, n),
        )

    def pass_on(wave, ci, way, half, hops, k):
        idx = ((way * k) % n) * 2 + half
        place = offsets[ci] + k - 1
        if wave == 0:
            wo_copy(way * k, half).wait()
        if k < hops:
            hop(wave, place + 1, way).wait_recv()

        @pl.loop(0, half_w // tile)
        def _(i):
            cols = pl.ds(pl.multiple_of(i * tile, tile), tile)
            value = nn_dot(ctx[wave * ws : (wave + 1) * ws, :], wo_b[idx, :, cols])
            if k < hops:
                value = value + rs_r[wave, place + 1, :, cols].astype(f32)
            rs_s[wave, place, :, cols] = value.astype(bf16)

        c = hop(wave, place, way)
        c.start()
        rs_sends.append((c, k))

    early = [x for x in sends if x[3] == x[4] == n // 2]
    lone = [x for x in sends if x[3] == x[4] != n // 2]
    joined = [x for x in sends if x[3] != x[4]]
    attend_wave(0)
    for x in early + lone:
        pass_on(0, *x)
    for wave in range(1, waves):
        attend_wave(wave)
        for x in early:
            pass_on(wave, *x)
        for x in joined:
            pass_on(wave - 1, *x)
        for x in lone:
            pass_on(wave, *x)

    settled(2)
    settled(3)
    down_t = jnp.concatenate([g_od[s] for s in range(reps)], axis=1)
    total_mid = nt_dot(ctx[...], down_t)
    mid_s[...] = total_mid.astype(bf16)
    mid_sends = []
    for j in range(1, n):
        c = remote(mid_s, mid_r.at[j], mid_ssem.at[j], mid_rsem.at[j], r, lax.rem(t + j, n))
        c.start()
        mid_sends.append(c)
    for x in joined:
        pass_on(waves - 1, *x)

    for c in mid_sends:
        c.wait_recv()
    for j in range(1, n):
        total_mid = total_mid + mid_r[j].astype(f32)
    middle = total_mid.astype(bf16)
    up_full = jnp.concatenate([g_ou[s] for s in range(reps)], axis=1)
    final = []
    for half in range(2):
        wo_copy(0, half).wait()
        final.append(
            nn_dot(ctx[...], wo_b[half])
            + adapter_scale * nn_dot(middle, up_full[:, half * half_w : (half + 1) * half_w])
        )
    for c, k in rs_sends:
        if k == 1:
            c.wait_recv()
    for half in range(2):
        value = final[half]
        for ci, (_way, h2, hops) in enumerate(channels_of(n)):
            if h2 == half and hops > 0:
                value = value + rs_r[:, offsets[ci]].reshape(seqs, half_w).astype(f32)
        out[:, half * half_w : (half + 1) * half_w] = value.astype(bf16)

    for c in dn_sends + dn_fwd + a_sends + g_sends + in_sends + mid_sends:
        c.wait_send()
    for c, _k in rs_sends:
        c.wait_send()


def local(
    hidden,
    norm_gain,
    query_weight_matrix,
    key_value_weight,
    output_weight_matrix,
    input_down_factors,
    query_up_factor,
    key_value_up_factors,
    output_down_factor,
    output_up_factor,
    cache_keys,
    cache_values,
    lengths,
):
    reps, n = lax.axis_size("rep"), lax.axis_size("tp")
    r, t = lax.axis_index("rep"), lax.axis_index("tp")
    seqs, depth = hidden.shape
    _, kv_local, cache, head_dim = cache_keys.shape
    width = query_weight_matrix.shape[1]
    heads = width // head_dim
    rank = input_down_factors.shape[2]
    block = input_down_factors.shape[1]
    win = max(block, LANES)

    down = jnp.swapaxes(input_down_factors, 1, 2).reshape(3 * rank, block)
    if win != block:
        spot = lax.rem((r * n + t) * block, win)
        down = lax.dynamic_update_slice(
            jnp.zeros((3 * rank, win), down.dtype), down, (0, spot)
        )
    f_q = query_up_factor
    f_kv = jnp.swapaxes(key_value_up_factors, 1, 2)
    f_od = output_down_factor.T
    f_ou = output_up_factor
    factors = (f_q, f_kv, f_od, f_ou)
    dims = dict(
        tp=n, rep=reps, rank=rank, block=block, win=win,
    )
    pad_heads = -(-heads // 8) * 8
    wide = depth // n
    half_w = wide // 2
    rows = seqs * pad_heads
    slots = sum(hops for _, _, hops in channels_of(n))
    steps, parts, waves = 16, 4, 2
    dma = pltpu.SemaphoreType.DMA
    hbm = pl.BlockSpec(memory_space=pl.ANY)
    vmem = pl.BlockSpec(memory_space=pltpu.VMEM)
    smem = pl.BlockSpec(memory_space=pltpu.SMEM)
    vec = pltpu.VMEM
    return pl.pallas_call(
        functools.partial(kernel, dims),
        name="decode_block",
        out_shape=jax.ShapeDtypeStruct((seqs, wide), bf16),
        in_specs=[hbm, vmem] + [hbm] * 10 + [smem],
        out_specs=vmem,
        scratch_shapes=[
            vec((seqs, depth), bf16),
            vec((seqs, depth), bf16),
            vec((depth, width), bf16),
            vec((2, depth, kv_local * head_dim), bf16),
            vec((2 * n, width, half_w), bf16),
            vec((seqs, kv_local, cache, head_dim), bf16),
            vec((seqs, kv_local, cache, head_dim), bf16),
            vec((reps, 3 * rank, win), bf16),
            *[vec((reps // 2,) + f.shape, bf16) for f in factors],
            *[vec((reps,) + f.shape, bf16) for f in factors],
            vec((seqs, head_dim), f32),
            vec((seqs, width), f32),
            vec((2, seqs, kv_local * head_dim), f32),
            vec((seqs, 3 * rank), f32),
            vec((seqs, 3 * rank), bf16),
            vec((n, seqs, 3 * rank), bf16),
            vec((rows, head_dim), f32),
            vec((rows, head_dim), f32),
            vec((rows, head_dim), f32),
            vec((rows, head_dim), f32),
            vec((seqs, width), bf16),
            vec((seqs, rank), bf16),
            vec((n, seqs, rank), bf16),
            vec((waves, slots, seqs // waves, half_w), bf16),
            vec((waves, slots, seqs // waves, half_w), bf16),
            dma,
            dma((steps,)),
            dma((steps,)),
            dma((2 * n,)),
            dma((parts,)),
            dma((parts,)),
            dma((1 + len(factors),)),
            dma((reps // 2,)),
            dma((reps,)),
            dma((reps // 2,)),
            dma((len(factors), reps // 2)),
            dma((len(factors), reps // 2)),
            dma((len(factors), reps)),
            dma((len(factors), reps)),
            dma((len(factors), reps)),
            dma((n,)),
            dma((n,)),
            dma((n,)),
            dma((n,)),
            dma((waves, slots)),
            dma((waves, slots)),
        ],
        compiler_params=pltpu.CompilerParams(
            collective_id=0, has_side_effects=True, vmem_limit_bytes=66000000
        ),
    )(
        hidden,
        norm_gain,
        query_weight_matrix,
        key_value_weight,
        output_weight_matrix,
        down,
        *factors,
        cache_keys,
        cache_values,
        lengths,
    )


def solution(mesh):
    return jax.shard_map(
        local,
        mesh=mesh,
        in_specs=(
            P("rep", None),
            P(),
            P(None, "tp"),
            P(None, None, "tp"),
            P("tp", None),
            P(None, ("rep", "tp"), None),
            P(None, ("rep", "tp")),
            P(None, None, ("rep", "tp")),
            P(("rep", "tp"), None),
            P(None, ("rep", "tp")),
            P("rep", "tp", None, None),
            P("rep", "tp", None, None),
            P("rep"),
        ),
        out_specs=P("rep", "tp"),
        check_vma=False,
    )
```

profile of v0, /device:TPU:0, one launch (start us, length us, event | category | flops | bytes accessed | tf_op | source)
XLA Modules:
  0.0 51.5 jit_solution(13229325851704873348)
XLA Ops:
  0.0 49.8 %decode_block.1 = bf16[64,2048]{1,0:T(8,128)(2,1)} custom-call(bf16[64,8192]{1,0:T(8,128)(2,1)} %hidden.1, bf16[8192]{0:T(1024)(128)(2,1)} %gain.1, bf16[8192,1024]{1,0:T(8,128)(2,1)} %wq.1, bf16[2,8192,256]{2,1,0:T(8,128)(2,1)} %wkv.1, bf16[1024,8192]{1,0:T(8,128)(2,1)} %wo.1, bf16[192,256]{1,0:T(8,128)(2,1)} %bitcast.5, bf16[64,128]{1,0:T(8,128)(2,1)} %f_q.1, ...), custom_call_target="tpu_custom_call" | custom-call | tf_op jit(solution)/shard_map/decode_block/pallas_call | solution.py:608
  49.8 1.7 %copy.15 = bf16[64,2048]{1,0:T(8,128)(2,1)} copy(bf16[64,2048]{1,0:T(8,128)(2,1)} %decode_block.1) | data formatting | bytes 524288
where the time goes:
time: 51.7 us; the launch traced here: 51.5 us
  Pallas kernels  49.8 us (96%)
  local copies, waits for them, and re-layouts  1.67 us (3%)
    pallas_call x1, Pallas kernels, local(): pl.pallas_call(functools.partial(kernel, dims), name='decode_block', out_...  49.8 us
    unnamed x1, local copies, waits for them, and re-layouts  1.67 us

commit v1 on v0

v1 whole, which is shorter than its diff:
```python
import functools
import math

import jax
import jax.numpy as jnp
from jax import lax
from jax.experimental import pallas as pl
from jax.experimental.pallas import tpu as pltpu
from jax.sharding import PartitionSpec as P

epsilon = 1e-06
rope_base = 1000000.0
adapter_scale = 0.5

f32 = jnp.float32
bf16 = jnp.bfloat16
LANES = 128
MESH_ID = pl.DeviceIdType.MESH


def nt_dot(left, right):
    return lax.dot_general(
        left, right, (((1,), (1,)), ((), ())), preferred_element_type=f32
    )


def nn_dot(left, right):
    return jnp.dot(left, right, preferred_element_type=f32)


def kernel(
    dims,
    hidden,
    gain,
    wq,
    wkv,
    wo,
    dn_own,
    f_q,
    f_kv,
    f_od,
    f_ou,
    cache_k,
    cache_v,
    lengths,
    out,
    gain_b,
    len_b,
    hid_b,
    norm_b,
    wq_b,
    wkv_b,
    wo_b,
    k_b,
    v_b,
    dn_b,
    a_q,
    a_kv,
    a_od,
    a_ou,
    g_q,
    g_kv,
    g_od,
    g_ou,
    angle,
    q_acc,
    kv_acc,
    inner_s,
    inner_r,
    q3,
    nk3,
    nv3,
    c3,
    top3,
    sum3,
    ctx,
    mid_s,
    mid_r,
    part_f,
    own_acc,
    rs_s,
    rs_r,
    small_sem,
    hid_sem,
    w_sem,
    kv_sem,
    wo_sem,
    k_sem,
    v_sem,
    own_sem,
    dn_ssem,
    dn_rsem,
    dn_fsem,
    a_ssem,
    a_rsem,
    g_ssem,
    g_rsem,
    g_fsem,
    in_ssem,
    in_rsem,
    mid_ssem,
    mid_rsem,
    rs_ssem,
    rs_rsem,
):
    n, reps = dims["tp"], dims["rep"]
    seqs, depth = hidden.shape
    head_dim = cache_k.shape[3]
    kv_local = cache_k.shape[1]
    heads = wq.shape[1] // head_dim
    group = heads // kv_local
    pad_heads = q3.shape[0] // seqs
    rank = dims["rank"]
    block, win = dims["block"], dims["win"]
    half_reps = reps // 2
    r = lax.axis_index("rep")
    t = lax.axis_index("tp")
    core = lax.rem(r, 2)
    partner = r + 1 - 2 * core

    barrier = pltpu.get_barrier_semaphore()

    def greet(rr, tt):
        pl.semaphore_signal(barrier, inc=1, device_id=(rr, tt), device_id_type=MESH_ID)

    count = 0
    for j in range(n - 1, 0, -1):
        greet(r, lax.rem(t + j, n))
        count += 1
    for j in range(1, half_reps):
        greet(lax.rem(r + 2 * j, reps), t)
        count += 1
    greet(partner, t)
    count += 1

    hid = pltpu.make_async_copy(hidden, hid_b, hid_sem)
    hid.start()
    gain_in = pltpu.make_async_copy(gain, gain_b, small_sem.at[0])
    gain_in.start()
    len_in = pltpu.make_async_copy(lengths, len_b, small_sem.at[1])
    len_in.start()
    own_dn = pltpu.make_async_copy(dn_own, dn_b.at[r], own_sem.at[0])
    mine_at = r // 2
    spread = (a_q, a_kv, a_od, a_ou)
    gathered = (g_q, g_kv, g_od, g_ou)
    own_f = [
        pltpu.make_async_copy(src, dst.at[mine_at], own_sem.at[1 + f])
        for f, (src, dst) in enumerate(zip((f_q, f_kv, f_od, f_ou), spread))
    ]
    own_dn.start()
    for c in own_f:
        c.start()
    steps = w_sem.shape[0]
    kc = depth // steps

    def w_copies(i):
        rows = pl.ds(pl.multiple_of(i * kc, kc), kc)
        return (
            pltpu.make_async_copy(wq.at[rows, :], wq_b.at[rows, :], w_sem.at[i]),
            pltpu.make_async_copy(wkv.at[:, rows, :], wkv_b.at[:, rows, :], kv_sem.at[i]),
        )

    @pl.loop(0, steps)
    def _(i):
        for c in w_copies(i):
            c.start()

    parts = k_sem.shape[0]
    ps = seqs // parts

    def cache_copies(i):
        rows = pl.ds(i * ps, ps)
        return (
            pltpu.make_async_copy(cache_k.at[rows], k_b.at[rows], k_sem.at[i]),
            pltpu.make_async_copy(cache_v.at[rows], v_b.at[rows], v_sem.at[i]),
        )

    wide = wo.shape[1] // n
    most, least = jnp.maximum(n - 1 - t, t), jnp.minimum(n - 1 - t, t)
    toward = jnp.where(n - 1 - t > t, 1, -1)

    def dest(i):
        lead = most - least
        late = jnp.maximum(i - lead, 0)
        away = least - late // 2
        side = jnp.where(late % 2 == 0, -toward, toward)
        return t + jnp.where(i < lead, toward * (most - i), side * away)

    def wo_copy(d):
        cols = pl.ds(pl.multiple_of(d * wide, LANES), wide)
        return pltpu.make_async_copy(wo.at[:, cols], wo_b.at[d], wo_sem.at[d])

    @pl.loop(0, parts)
    def _(i):
        for c in cache_copies(i):
            c.start()

    @pl.loop(0, n - 1)
    def _(i):
        wo_copy(dest(i)).start()

    wo_copy(t).start()

    def remote(src, dst, ssem, rsem, rr, tt):
        return pltpu.make_async_remote_copy(
            src_ref=src,
            dst_ref=dst,
            send_sem=ssem,
            recv_sem=rsem,
            device_id=(rr, tt),
            device_id_type=MESH_ID,
        )

    pl.semaphore_wait(barrier, count)
    ranks = (pl.ds(0, rank), pl.ds(rank, 2 * rank))
    dn_sends = []

    def down(src, part, ssem, rr):
        here = dn_b.at[src, ranks[part]]
        return remote(here, here, ssem, dn_rsem.at[part, src], rr, t)

    def send_down(part):
        for j in range(1, half_reps):
            dn_sends.append(down(r, part, dn_ssem.at[part, j], lax.rem(r + 2 * j, reps)))
        dn_sends.append(down(r, part, dn_fsem.at[part, 0], partner))
        for c in dn_sends[-half_reps:]:
            c.start()

    def relay_down(part):
        for j in range(half_reps - 1, 0, -1):
            src = lax.rem(r + 2 * j, reps)
            c = down(src, part, dn_fsem.at[part, j], partner)
            c.wait_recv()
            c.start()
            dn_sends.append(c)

    def share_inner(part):
        for j in range(half_reps):
            src = lax.rem(partner + 2 * j, reps)
            down(src, part, dn_fsem.at[part, j], partner).wait_recv()
        total = jnp.zeros((seqs, (1 + part) * rank), f32)
        for j in range(reps):
            start = (j * n + t) * block
            cols = pl.ds(pl.multiple_of(start // win * win, LANES), win)
            total = total + nt_dot(norm_b[:, cols], dn_b[j, ranks[part]])
        sends = share(
            packed(total), inner_s.at[part], inner_r.at[part], in_ssem.at[part], in_rsem.at[part]
        )
        return sends, total

    fold = max(1, LANES // rank)
    few = seqs // fold

    def packed(x):
        if x.shape[1] != rank:
            return x
        return jnp.concatenate([x[f * few : (f + 1) * few] for f in range(fold)], axis=1)

    def unpacked(x):
        return jnp.concatenate([x[:, f * rank : (f + 1) * rank] for f in range(fold)], axis=0)

    def share(x, own, others, ssem, rsem):
        size = x.shape[0]
        own[pl.ds(0, size), :] = x.astype(bf16)
        made = []
        for j in range(1, n):
            c = remote(
                own.at[pl.ds(0, size)], others.at[j, pl.ds(0, size)], ssem.at[j], rsem.at[j],
                r, lax.rem(t + j, n),
            )
            c.start()
            made.append(c)
        return made

    def gather_sum(total, sends, others):
        for c in sends:
            c.wait_recv()
        for j in range(1, n):
            got = others[j] if total.shape[1] != rank else unpacked(others[j, :few])
            total = total + got.astype(f32)
        return total.astype(bf16)

    a_sends = []

    def to_chips(f):
        buf = spread[f]
        own_f[f].wait()
        for j in range(1, half_reps):
            c = remote(
                buf.at[mine_at], buf.at[mine_at], a_ssem.at[f, j], a_rsem.at[f, mine_at],
                lax.rem(r + 2 * j, reps), t,
            )
            c.start()
            a_sends.append(c)

    per_plane = reps // n
    groups = per_plane // 2
    g_sends = []

    def to_planes(f):
        buf, full = spread[f], gathered[f]
        for j in range(1, half_reps):
            src = lax.rem(r + 2 * j, reps) // 2
            remote(
                buf.at[src], buf.at[src], a_ssem.at[f, j], a_rsem.at[f, src], r, t
            ).wait_recv()
        for i in range(groups):
            s = n * (2 * i + core) + t
            for j in range(1, n):
                plane = lax.rem(t + j, n)
                src = (plane * per_plane + 2 * i) // 2
                c = remote(
                    buf.at[src], full.at[s], g_ssem.at[f, i * n + j], g_rsem.at[f, s],
                    r, plane,
                )
                c.start()
                g_sends.append(c)
            src = (t * per_plane + 2 * i) // 2
            pltpu.make_async_copy(buf.at[src], full.at[s], g_rsem.at[f, s]).start()

    def across(f):
        full = gathered[f]
        for i in range(groups):
            for z in range(n):
                s = n * (2 * i + core) + z
                pltpu.make_async_copy(spread[f].at[0], full.at[s], g_rsem.at[f, s]).wait()
                c = remote(
                    full.at[s], full.at[s], g_fsem.at[f, i * n + z], g_rsem.at[f, s],
                    partner, t,
                )
                c.start()
                g_sends.append(c)

    def settled(f):
        full = gathered[f]
        for i in range(groups):
            for z in range(n):
                s = n * (2 * i + 1 - core) + z
                pltpu.make_async_copy(spread[f].at[0], full.at[s], g_rsem.at[f, s]).wait()

    to_chips(0)
    own_dn.wait()
    send_down(0)
    to_chips(1)
    send_down(1)
    to_chips(2)
    to_chips(3)

    gain_in.wait()
    hid.wait()

    @pl.loop(0, seqs // 16)
    def _(i):
        rows = pl.ds(pl.multiple_of(i * 16, 16), 16)
        x = hid_b[rows, :].astype(f32)
        square = jnp.mean(x * x, axis=-1, keepdims=True)
        norm_b[rows, :] = (
            x * lax.rsqrt(square + epsilon) * gain_b[...].astype(f32).reshape(1, depth)
        ).astype(bf16)

    q_acc[...] = jnp.zeros_like(q_acc)
    kv_acc[...] = jnp.zeros_like(kv_acc)
    both = 2 * kc

    def project(lo, hi):
        @pl.loop(lo, hi)
        def _(i):
            for j in range(2):
                for c in w_copies(2 * i + j):
                    c.wait()
            rows = pl.ds(pl.multiple_of(i * both, both), both)
            x = norm_b[:, rows]
            q_acc[...] += nn_dot(x, wq_b[rows, :])
            for j in range(2):
                kv_acc[j] += nn_dot(x, wkv_b[j, rows, :])

    project(0, 3)
    to_planes(0)
    project(3, 5)
    relay_down(0)
    project(5, 6)
    to_planes(1)
    q_sends, q_part = share_inner(0)
    project(6, 8)
    len_in.wait()

    half_dim = head_dim // 2
    step = lax.rem(lax.broadcasted_iota(jnp.int32, (1, head_dim), 1), half_dim)
    frequency = jnp.exp(step.astype(f32) * (-2.0 * math.log(rope_base) / head_dim))

    @pl.loop(0, seqs // 8)
    def _(i):
        for b in range(8):
            angle[pl.ds(i * 8 + b, 1), :] = len_b[i * 8 + b].astype(f32) * frequency

    cosv = jnp.cos(angle[...])
    sinv = jnp.sin(angle[...])
    lane = lax.broadcasted_iota(jnp.int32, (seqs, head_dim), 1)
    sinv = jnp.where(lane < half_dim, -sinv, sinv)

    def turn(x):
        return x * cosv + pltpu.roll(x, head_dim // 2, 1) * sinv

    across(0)
    relay_down(1)
    across(1)
    kv_sends, kv_part = share_inner(1)
    settled(0)
    inner_q = gather_sum(q_part, q_sends, inner_r.at[0])
    q_up = jnp.concatenate([g_q[s] for s in range(reps)], axis=1)
    q = q_acc[...] + adapter_scale * nn_dot(inner_q, q_up)
    for h in range(pad_heads):
        rows = pl.ds(h, seqs, stride=pad_heads)
        if h < heads:
            q3[rows, :] = turn(q[:, h * head_dim : (h + 1) * head_dim])
        else:
            q3[rows, :] = jnp.zeros((seqs, head_dim), f32)

    def rows_of(j):
        w = g_kv.shape[2]
        return g_kv[:, j].astype(f32).reshape(reps * w, rank).astype(bf16)

    def new_pair():
        inner = gather_sum(kv_part, kv_sends, inner_r.at[1]).astype(f32)
        inner_k = inner[:, :rank].astype(bf16)
        inner_v = inner[:, rank:].astype(bf16)
        nk = kv_acc[0] + adapter_scale * nt_dot(inner_k, rows_of(0))
        nv = kv_acc[1] + adapter_scale * nt_dot(inner_v, rows_of(1))
        for j in range(kv_local):
            key = turn(nk[:, j * head_dim : (j + 1) * head_dim]).astype(bf16).astype(f32)
            val = nv[:, j * head_dim : (j + 1) * head_dim].astype(bf16).astype(f32)
            for g in range(pad_heads):
                if min(g // group, kv_local - 1) == j:
                    rows = pl.ds(g, seqs, stride=pad_heads)
                    nk3[rows, :] = key
                    nv3[rows, :] = val

    cache = cache_k.shape[2]
    span = kv_local * cache
    score_scale = 1.0 / math.sqrt(head_dim)
    bs = min(16, ps)
    per = ps // bs

    def attend(i):
        @pl.when(lax.rem(i, per) == 0)
        def _():
            for c in cache_copies(i // per):
                c.wait()

        base = pl.multiple_of(i * (bs * pad_heads), bs * pad_heads)
        rows = pl.ds(base, bs * pad_heads)
        qq = q3[rows, :]
        hi = qq.astype(bf16).astype(f32)
        rest = qq - hi
        mid = rest.astype(bf16).astype(f32)
        low = rest - mid
        row_id = lax.broadcasted_iota(jnp.int32, (pad_heads, span), 0)
        col_id = lax.broadcasted_iota(jnp.int32, (pad_heads, span), 1)
        mine = jnp.minimum(row_id // group, kv_local - 1) == col_id // cache
        pos = lax.rem(col_id, cache)
        scored = []
        for b in range(bs):
            sl = slice(b * pad_heads, (b + 1) * pad_heads)
            stack = jnp.concatenate([hi[sl], mid[sl], low[sl]], axis=0).astype(bf16)
            keys = k_b[i * bs + b].reshape(span, head_dim)
            dots = nt_dot(stack, keys)
            sc = (
                dots[:pad_heads]
                + dots[pad_heads : 2 * pad_heads]
                + dots[2 * pad_heads :]
            ) * score_scale
            live = jnp.logical_and(mine, pos < len_b[i * bs + b])
            scored.append(jnp.where(live, sc, -1e30))
        sc = jnp.concatenate(scored, axis=0)
        top = jnp.max(sc, axis=-1, keepdims=True)
        w = jnp.exp(sc - top)
        top3[rows, :] = jnp.broadcast_to(top, (bs * pad_heads, head_dim))
        sum3[rows, :] = jnp.broadcast_to(
            jnp.sum(w, axis=-1, keepdims=True), (bs * pad_heads, head_dim)
        )
        for b in range(bs):
            sl = slice(b * pad_heads, (b + 1) * pad_heads)
            vals = v_b[i * bs + b].reshape(span, head_dim)
            here = pl.ds(base + b * pad_heads, pad_heads)
            c3[here, :] = nn_dot(w[sl].astype(bf16), vals)

    def merge(i):
        rows = pl.ds(i * (bs * pad_heads), bs * pad_heads)
        own = jnp.sum(q3[rows, :] * nk3[rows, :], axis=-1, keepdims=True) * score_scale
        top = jnp.maximum(top3[rows, :], own)
        old = jnp.exp(top3[rows, :] - top)
        new = jnp.exp(own - top)
        scale = 1.0 / (sum3[rows, :] * old + new)
        c3[rows, :] = c3[rows, :] * (old * scale) + (new * scale).astype(bf16).astype(
            f32
        ) * nv3[rows, :]

    waves = rs_ssem.shape[1]
    ws = seqs // waves
    tile = min(1024, wide)

    def finish_wave(wave):
        for i in range(wave * ws // bs, (wave + 1) * ws // bs):
            merge(i)
        for h in range(heads):
            ctx[wave * ws : (wave + 1) * ws, h * head_dim : (h + 1) * head_dim] = c3[
                pl.ds(wave * ws * pad_heads + h, ws, stride=pad_heads), :
            ].astype(bf16)

    def hop(d, wave, up):
        rows = pl.ds(pl.multiple_of(wave * ws, ws), ws)
        slot = d + up
        return remote(
            rs_s.at[d, rows], rs_r.at[slot, rows], rs_ssem.at[d, wave],
            rs_rsem.at[slot, wave], r, t + 2 * up - 1,
        )

    def pass_on(i, wave):
        d = dest(i)
        up = jnp.where(d > t, 1, 0)
        rows = pl.ds(pl.multiple_of(wave * ws, ws), ws)
        for j in range(wide // tile):
            cols = slice(j * tile, (j + 1) * tile)
            part_f[:, cols] = nn_dot(ctx[rows, :], wo_b[d, :, cols])
        fed = jnp.where(d > t, t > 0, t < n - 1)

        @pl.when(fed)
        def _():
            hop(d, wave, up).wait_recv()
            rs_s[d, rows, :] = (part_f[...] + rs_r[d + up, rows, :].astype(f32)).astype(bf16)

        @pl.when(jnp.logical_not(fed))
        def _():
            rs_s[d, rows, :] = part_f[...].astype(bf16)

        hop(d, wave, up).start()

    pl.loop(0, seqs // bs)(attend)
    to_planes(2)
    to_planes(3)
    settled(1)
    new_pair()
    at_end = jnp.logical_or(t == 0, t == n - 1)
    for wave in range(waves):
        finish_wave(wave)
        if wave == 0:
            wo_copy(dest(0)).wait()

        @pl.when(at_end)
        def _():
            pass_on(0, wave)

    across(2)
    settled(2)
    down_t = jnp.concatenate([g_od[s] for s in range(reps)], axis=1)
    mid_part = nt_dot(ctx[...], down_t)
    mid_sends = share(packed(mid_part), mid_s, mid_r, mid_ssem, mid_rsem)
    across(3)

    @pl.loop(jnp.where(at_end, 1, 0), n - 1)
    def _(i):
        @pl.when(i > 0)
        def _():
            wo_copy(dest(i)).wait()

        @pl.loop(0, waves)
        def _(wave):
            pass_on(i, wave)

    wo_copy(t).wait()
    for j in range(wide // tile):
        cols = slice(j * tile, (j + 1) * tile)
        own_acc[:, cols] = nn_dot(ctx[...], wo_b[t, :, cols])
    settled(3)
    middle = gather_sum(mid_part, mid_sends, mid_r)
    up_full = jnp.concatenate([g_ou[s] for s in range(reps)], axis=1)
    own_acc[...] += adapter_scale * nn_dot(middle, up_full)

    @pl.loop(0, waves)
    def _(wave):
        rows = pl.ds(pl.multiple_of(wave * ws, ws), ws)

        @pl.when(t < n - 1)
        def _():
            hop(t, wave, 0).wait_recv()
            own_acc[rows, :] += rs_r[t, rows, :].astype(f32)

        @pl.when(t > 0)
        def _():
            hop(t, wave, 1).wait_recv()
            own_acc[rows, :] += rs_r[t + 1, rows, :].astype(f32)

        out[rows, :] = own_acc[rows, :].astype(bf16)

    for c in dn_sends + a_sends + g_sends + q_sends + kv_sends + mid_sends:
        c.wait_send()

    @pl.loop(0, n - 1)
    def _(i):
        d = dest(i)

        @pl.loop(0, waves)
        def _(wave):
            hop(d, wave, jnp.where(d > t, 1, 0)).wait_send()


def local(
    hidden,
    norm_gain,
    query_weight_matrix,
    key_value_weight,
    output_weight_matrix,
    input_down_factors,
    query_up_factor,
    key_value_up_factors,
    output_down_factor,
    output_up_factor,
    cache_keys,
    cache_values,
    lengths,
):
    reps, n = lax.axis_size("rep"), lax.axis_size("tp")
    r, t = lax.axis_index("rep"), lax.axis_index("tp")
    seqs, depth = hidden.shape
    _, kv_local, cache, head_dim = cache_keys.shape
    width = query_weight_matrix.shape[1]
    heads = width // head_dim
    rank = input_down_factors.shape[2]
    block = input_down_factors.shape[1]
    win = max(block, LANES)

    down = jnp.swapaxes(input_down_factors, 1, 2).reshape(3 * rank, block)
    if win != block:
        spot = lax.rem((r * n + t) * block, win)
        down = lax.dynamic_update_slice(
            jnp.zeros((3 * rank, win), down.dtype), down, (0, spot)
        )
    f_q = query_up_factor
    f_kv = jnp.swapaxes(key_value_up_factors, 1, 2)
    f_od = output_down_factor.T
    f_ou = output_up_factor
    factors = (f_q, f_kv, f_od, f_ou)
    dims = dict(
        tp=n, rep=reps, rank=rank, block=block, win=win,
    )
    pad_heads = -(-heads // 8) * 8
    wide = depth // n
    rows = seqs * pad_heads
    steps, parts, waves = 16, 4, seqs // 16
    dma = pltpu.SemaphoreType.DMA
    hbm = pl.BlockSpec(memory_space=pl.ANY)
    vmem = pl.BlockSpec(memory_space=pltpu.VMEM)
    vec = pltpu.VMEM
    return pl.pallas_call(
        functools.partial(kernel, dims),
        name="decode_block",
        out_shape=jax.ShapeDtypeStruct((seqs, wide), bf16),
        in_specs=[hbm] * 13,
        out_specs=vmem,
        scratch_shapes=[
            vec((depth,), bf16),
            pltpu.SMEM((seqs,), jnp.int32),
            vec((seqs, depth), bf16),
            vec((seqs, depth), bf16),
            vec((depth, width), bf16),
            vec((2, depth, kv_local * head_dim), bf16),
            vec((n, width, wide), bf16),
            vec((seqs, kv_local, cache, head_dim), bf16),
            vec((seqs, kv_local, cache, head_dim), bf16),
            vec((reps, 3 * rank, win), bf16),
            *[vec((reps // 2,) + f.shape, bf16) for f in factors],
            *[vec((reps,) + f.shape, bf16) for f in factors],
            vec((seqs, head_dim), f32),
            vec((seqs, width), f32),
            vec((2, seqs, kv_local * head_dim), f32),
            vec((2, seqs, 2 * rank), bf16),
            vec((2, n, seqs, 2 * rank), bf16),
            *[vec((rows, head_dim), f32)] * 6,
            vec((seqs, width), bf16),
            vec((seqs, 2 * rank), bf16),
            vec((n, seqs, 2 * rank), bf16),
            vec((seqs // waves, wide), f32),
            vec((seqs, wide), f32),
            vec((n, seqs, wide), bf16),
            vec((n + 1, seqs, wide), bf16),
            dma((2,)),
            dma,
            dma((steps,)),
            dma((steps,)),
            dma((n,)),
            dma((parts,)),
            dma((parts,)),
            dma((1 + len(factors),)),
            dma((2, reps // 2)),
            dma((2, reps)),
            dma((2, reps // 2)),
            dma((len(factors), reps // 2)),
            dma((len(factors), reps // 2)),
            dma((len(factors), reps)),
            dma((len(factors), reps)),
            dma((len(factors), reps)),
            dma((2, n)),
            dma((2, n)),
            dma((n,)),
            dma((n,)),
            dma((n, waves)),
            dma((n + 1, waves)),
        ],
        compiler_params=pltpu.CompilerParams(
            collective_id=0, has_side_effects=True, vmem_limit_bytes=66000000
        ),
    )(
        hidden,
        norm_gain,
        query_weight_matrix,
        key_value_weight,
        output_weight_matrix,
        down,
        *factors,
        cache_keys,
        cache_values,
        lengths,
    )


def solution(mesh):
    return jax.shard_map(
        local,
        mesh=mesh,
        in_specs=(
            P("rep", None),
            P(),
            P(None, "tp"),
            P(None, None, "tp"),
            P("tp", None),
            P(None, ("rep", "tp"), None),
            P(None, ("rep", "tp")),
            P(None, None, ("rep", "tp")),
            P(("rep", "tp"), None),
            P(None, ("rep", "tp")),
            P("rep", "tp", None, None),
            P("rep", "tp", None, None),
            P("rep"),
        ),
        out_specs=P("rep", "tp"),
        check_vma=False,
    )
```

time: 51.7 us -> 44.5 us (0.86)
  Pallas kernels: 49.8 us -> 42.7 us
    pallas_call x1, Pallas kernels: 49.8 us -> 42.7 us  [local(): pl.pallas_call(functools.partial(kernel, dims), name='decode_block', out_...]
where the time goes in v1:
time: 44.5 us; the launch traced here: 44.4 us
  Pallas kernels  42.7 us (96%)
  local copies, waits for them, and re-layouts  1.67 us (4%)
    pallas_call x1, Pallas kernels, local(): pl.pallas_call(functools.partial(kernel, dims), name='decode_block', out_...  42.7 us
    unnamed x1, local copies, waits for them, and re-layouts  1.67 us

profile of v1, /device:TPU:0, one launch (start us, length us, event | category | flops | bytes accessed | tf_op | source)
XLA Modules:
  0.0 44.4 jit_solution(16757672328371626362)
XLA Ops:
  0.0 42.7 %decode_block.1 = bf16[64,2048]{1,0:T(8,128)(2,1)} custom-call(bf16[64,8192]{1,0:T(8,128)(2,1)} %hidden.1, bf16[8192]{0:T(1024)(128)(2,1)} %gain.1, bf16[8192,1024]{1,0:T(8,128)(2,1)} %wq.1, bf16[2,8192,256]{2,1,0:T(8,128)(2,1)} %wkv.1, bf16[1024,8192]{1,0:T(8,128)(2,1)} %wo.1, bf16[192,256]{1,0:T(8,128)(2,1)} %bitcast.5, bf16[64,128]{1,0:T(8,128)(2,1)} %f_q.1, ...), custom_call_target="tpu_custom_call" | custom-call | tf_op jit(solution)/shard_map/decode_block/pallas_call | solution.py:654
  42.7 1.7 %copy.15 = bf16[64,2048]{1,0:T(8,128)(2,1)} copy(bf16[64,2048]{1,0:T(8,128)(2,1)} %decode_block.1) | data formatting | bytes 524288

commit v2 on v1

--- a/solution.py
+++ b/solution.py
@@ -90,7 +90,6 @@
     own_sem,
     dn_ssem,
     dn_rsem,
-    dn_fsem,
     a_ssem,
     a_rsem,
     g_ssem,
@@ -102,6 +101,7 @@
     mid_rsem,
     rs_ssem,
     rs_rsem,
+    ready,
 ):
     n, reps = dims["tp"], dims["rep"]
     seqs, depth = hidden.shape
@@ -124,12 +124,21 @@
         pl.semaphore_signal(barrier, inc=1, device_id=(rr, tt), device_id_type=MESH_ID)
 
     count = 0
-    for j in range(n - 1, 0, -1):
-        greet(r, lax.rem(t + j, n))
-        count += 1
+    below, above = t > 0, t < n - 1
+
+    @pl.when(below)
+    def _():
+        greet(r, t - 1)
+
+    @pl.when(above)
+    def _():
+        greet(r, t + 1)
+
+    beside = jnp.where(below, 1, 0) + jnp.where(above, 1, 0)
     for j in range(1, half_reps):
         greet(lax.rem(r + 2 * j, reps), t)
-        count += 1
+        greet(lax.rem(partner + 2 * j, reps), t)
+        count += 2
     greet(partner, t)
     count += 1
 
@@ -211,42 +220,50 @@
             device_id_type=MESH_ID,
         )
 
-    pl.semaphore_wait(barrier, count)
+    pl.semaphore_wait(barrier, count + beside)
+
+    def tell(k):
+        @pl.when(below)
+        def _():
+            pl.semaphore_signal(
+                ready.at[k], inc=1, device_id=(r, t - 1), device_id_type=MESH_ID
+            )
+
+        @pl.when(above)
+        def _():
+            pl.semaphore_signal(
+                ready.at[k], inc=1, device_id=(r, t + 1), device_id_type=MESH_ID
+            )
+
+    tell(0)
     ranks = (pl.ds(0, rank), pl.ds(rank, 2 * rank))
-    dn_sends = []
-
-    def down(src, part, ssem, rr):
+
+    def whole(ref, sem):
+        return pltpu.make_async_copy(ref, ref, sem)
+
+    def down(src, part, way, rr):
         here = dn_b.at[src, ranks[part]]
-        return remote(here, here, ssem, dn_rsem.at[part, src], rr, t)
+        return remote(here, here, dn_ssem.at[part], dn_rsem.at[part, way], rr, t)
 
     def send_down(part):
         for j in range(1, half_reps):
-            dn_sends.append(down(r, part, dn_ssem.at[part, j], lax.rem(r + 2 * j, reps)))
-        dn_sends.append(down(r, part, dn_fsem.at[part, 0], partner))
-        for c in dn_sends[-half_reps:]:
-            c.start()
+            down(r, part, 0, lax.rem(partner + 2 * j, reps)).start()
+        down(r, part, 1, partner).start()
 
     def relay_down(part):
-        for j in range(half_reps - 1, 0, -1):
-            src = lax.rem(r + 2 * j, reps)
-            c = down(src, part, dn_fsem.at[part, j], partner)
-            c.wait_recv()
-            c.start()
-            dn_sends.append(c)
+        whole(dn_b.at[pl.ds(0, half_reps - 1), ranks[part]], dn_rsem.at[part, 0]).wait()
+        for j in range(1, half_reps):
+            down(lax.rem(partner + 2 * j, reps), part, 1, partner).start()
 
     def share_inner(part):
-        for j in range(half_reps):
-            src = lax.rem(partner + 2 * j, reps)
-            down(src, part, dn_fsem.at[part, j], partner).wait_recv()
+        whole(dn_b.at[pl.ds(0, half_reps), ranks[part]], dn_rsem.at[part, 1]).wait()
         total = jnp.zeros((seqs, (1 + part) * rank), f32)
         for j in range(reps):
             start = (j * n + t) * block
             cols = pl.ds(pl.multiple_of(start // win * win, LANES), win)
             total = total + nt_dot(norm_b[:, cols], dn_b[j, ranks[part]])
-        sends = share(
-            packed(total), inner_s.at[part], inner_r.at[part], in_ssem.at[part], in_rsem.at[part]
-        )
-        return sends, total
+        share(packed(total), inner_s.at[part], inner_r.at[part], in_ssem.at[part], in_rsem.at[part])
+        return total
 
     fold = max(1, LANES // rank)
     few = seqs // fold
@@ -262,81 +279,57 @@
     def share(x, own, others, ssem, rsem):
         size = x.shape[0]
         own[pl.ds(0, size), :] = x.astype(bf16)
-        made = []
         for j in range(1, n):
-            c = remote(
-                own.at[pl.ds(0, size)], others.at[j, pl.ds(0, size)], ssem.at[j], rsem.at[j],
+            remote(
+                own.at[pl.ds(0, size)], others.at[j, pl.ds(0, size)], ssem, rsem,
                 r, lax.rem(t + j, n),
-            )
-            c.start()
-            made.append(c)
-        return made
-
-    def gather_sum(total, sends, others):
-        for c in sends:
-            c.wait_recv()
+            ).start()
+
+    def shared(total, others, sem):
+        size = few if total.shape[1] == rank else seqs
+        return whole(others.at[pl.ds(0, n - 1), pl.ds(0, size)], sem)
+
+    def gather_sum(total, others, rsem):
+        shared(total, others, rsem).wait()
         for j in range(1, n):
             got = others[j] if total.shape[1] != rank else unpacked(others[j, :few])
             total = total + got.astype(f32)
         return total.astype(bf16)
 
-    a_sends = []
-
     def to_chips(f):
-        buf = spread[f]
+        here = spread[f].at[mine_at]
         own_f[f].wait()
         for j in range(1, half_reps):
-            c = remote(
-                buf.at[mine_at], buf.at[mine_at], a_ssem.at[f, j], a_rsem.at[f, mine_at],
-                lax.rem(r + 2 * j, reps), t,
-            )
-            c.start()
-            a_sends.append(c)
+            remote(
+                here, here, a_ssem.at[f], a_rsem.at[f], lax.rem(r + 2 * j, reps), t
+            ).start()
 
     per_plane = reps // n
     groups = per_plane // 2
-    g_sends = []
 
     def to_planes(f):
         buf, full = spread[f], gathered[f]
-        for j in range(1, half_reps):
-            src = lax.rem(r + 2 * j, reps) // 2
-            remote(
-                buf.at[src], buf.at[src], a_ssem.at[f, j], a_rsem.at[f, src], r, t
-            ).wait_recv()
+        whole(buf.at[pl.ds(0, half_reps - 1)], a_rsem.at[f]).wait()
         for i in range(groups):
             s = n * (2 * i + core) + t
             for j in range(1, n):
                 plane = lax.rem(t + j, n)
                 src = (plane * per_plane + 2 * i) // 2
-                c = remote(
-                    buf.at[src], full.at[s], g_ssem.at[f, i * n + j], g_rsem.at[f, s],
-                    r, plane,
-                )
-                c.start()
-                g_sends.append(c)
+                remote(
+                    buf.at[src], full.at[s], g_ssem.at[f], g_rsem.at[f, 0], r, plane
+                ).start()
             src = (t * per_plane + 2 * i) // 2
-            pltpu.make_async_copy(buf.at[src], full.at[s], g_rsem.at[f, s]).start()
+            pltpu.make_async_copy(buf.at[src], full.at[s], g_rsem.at[f, 0]).start()
 
     def across(f):
         full = gathered[f]
+        whole(full.at[pl.ds(0, groups * n)], g_rsem.at[f, 0]).wait()
         for i in range(groups):
-            for z in range(n):
-                s = n * (2 * i + core) + z
-                pltpu.make_async_copy(spread[f].at[0], full.at[s], g_rsem.at[f, s]).wait()
-                c = remote(
-                    full.at[s], full.at[s], g_fsem.at[f, i * n + z], g_rsem.at[f, s],
-                    partner, t,
-                )
-                c.start()
-                g_sends.append(c)
+            here = full.at[pl.ds(n * (2 * i + core), n)]
+            remote(here, here, g_fsem.at[f], g_rsem.at[f, 1], partner, t).start()
 
     def settled(f):
-        full = gathered[f]
-        for i in range(groups):
-            for z in range(n):
-                s = n * (2 * i + 1 - core) + z
-                pltpu.make_async_copy(spread[f].at[0], full.at[s], g_rsem.at[f, s]).wait()
+        whole(gathered[f].at[pl.ds(0, groups * n)], g_rsem.at[f, 1]).wait()
 
     to_chips(0)
     own_dn.wait()
@@ -360,28 +353,36 @@
 
     q_acc[...] = jnp.zeros_like(q_acc)
     kv_acc[...] = jnp.zeros_like(kv_acc)
-    both = 2 * kc
-
-    def project(lo, hi):
-        @pl.loop(lo, hi)
-        def _(i):
-            for j in range(2):
-                for c in w_copies(2 * i + j):
-                    c.wait()
-            rows = pl.ds(pl.multiple_of(i * both, both), both)
-            x = norm_b[:, rows]
-            q_acc[...] += nn_dot(x, wq_b[rows, :])
-            for j in range(2):
-                kv_acc[j] += nn_dot(x, wkv_b[j, rows, :])
-
-    project(0, 3)
+
+    def project(i, many):
+        for j in range(many):
+            for c in w_copies(i + j):
+                c.wait()
+        rows = pl.ds(pl.multiple_of(i * kc, kc), many * kc)
+        x = norm_b[:, rows]
+        q_acc[...] += nn_dot(x, wq_b[rows, :])
+        for j in range(2):
+            kv_acc[j] += nn_dot(x, wkv_b[j, rows, :])
+
+    def heard(k):
+        if k < n - 2:
+            pl.semaphore_wait(ready.at[k], beside)
+        if k < n - 3:
+            tell(k + 1)
+
+    project(0, 2)
+    heard(0)
+    project(2, 2)
+    for k in range(1, n - 2):
+        heard(k)
     to_planes(0)
-    project(3, 5)
+    project(4, 1)
     relay_down(0)
-    project(5, 6)
+    project(5, 1)
+    q_part = share_inner(0)
+    project(6, 2)
     to_planes(1)
-    q_sends, q_part = share_inner(0)
-    project(6, 8)
+    relay_down(1)
     len_in.wait()
 
     half_dim = head_dim // 2
@@ -402,11 +403,9 @@
         return x * cosv + pltpu.roll(x, head_dim // 2, 1) * sinv
 
     across(0)
-    relay_down(1)
-    across(1)
-    kv_sends, kv_part = share_inner(1)
+    kv_part = share_inner(1)
     settled(0)
-    inner_q = gather_sum(q_part, q_sends, inner_r.at[0])
+    inner_q = gather_sum(q_part, inner_r.at[0], in_rsem.at[0])
     q_up = jnp.concatenate([g_q[s] for s in range(reps)], axis=1)
     q = q_acc[...] + adapter_scale * nn_dot(inner_q, q_up)
     for h in range(pad_heads):
@@ -421,7 +420,7 @@
         return g_kv[:, j].astype(f32).reshape(reps * w, rank).astype(bf16)
 
     def new_pair():
-        inner = gather_sum(kv_part, kv_sends, inner_r.at[1]).astype(f32)
+        inner = gather_sum(kv_part, inner_r.at[1], in_rsem.at[1]).astype(f32)
         inner_k = inner[:, :rank].astype(bf16)
         inner_v = inner[:, rank:].astype(bf16)
         nk = kv_acc[0] + adapter_scale * nt_dot(inner_k, rows_of(0))
@@ -495,8 +494,6 @@
             f32
         ) * nv3[rows, :]
 
-    waves = rs_ssem.shape[1]
-    ws = seqs // waves
     tile = min(1024, wide)
 
     def finish_wave(wave):
@@ -511,7 +508,7 @@
         rows = pl.ds(pl.multiple_of(wave * ws, ws), ws)
         slot = d + up
         return remote(
-            rs_s.at[d, rows], rs_r.at[slot, rows], rs_ssem.at[d, wave],
+            rs_s.at[d, rows], rs_r.at[slot, rows], rs_ssem,
             rs_rsem.at[slot, wave], r, t + 2 * up - 1,
         )
 
@@ -535,13 +532,21 @@
 
         hop(d, wave, up).start()
 
-    pl.loop(0, seqs // bs)(attend)
+    waves = rs_rsem.shape[1]
+    ws = seqs // waves
+    blocks = ws // bs
+    ahead = min(2, waves)
+    pl.loop(0, blocks)(attend)
+    across(1)
     to_planes(2)
     to_planes(3)
+    pl.loop(blocks, ahead * blocks)(attend)
     settled(1)
     new_pair()
     at_end = jnp.logical_or(t == 0, t == n - 1)
     for wave in range(waves):
+        if wave >= ahead:
+            pl.loop(wave * blocks, (wave + 1) * blocks)(attend)
         finish_wave(wave)
         if wave == 0:
             wo_copy(dest(0)).wait()
@@ -554,8 +559,7 @@
     settled(2)
     down_t = jnp.concatenate([g_od[s] for s in range(reps)], axis=1)
     mid_part = nt_dot(ctx[...], down_t)
-    mid_sends = share(packed(mid_part), mid_s, mid_r, mid_ssem, mid_rsem)
-    across(3)
+    share(packed(mid_part), mid_s, mid_r, mid_ssem, mid_rsem)
 
     @pl.loop(jnp.where(at_end, 1, 0), n - 1)
     def _(i):
@@ -567,12 +571,13 @@
         def _(wave):
             pass_on(i, wave)
 
+    across(3)
     wo_copy(t).wait()
     for j in range(wide // tile):
         cols = slice(j * tile, (j + 1) * tile)
         own_acc[:, cols] = nn_dot(ctx[...], wo_b[t, :, cols])
     settled(3)
-    middle = gather_sum(mid_part, mid_sends, mid_r)
+    middle = gather_sum(mid_part, mid_r, mid_rsem)
     up_full = jnp.concatenate([g_ou[s] for s in range(reps)], axis=1)
     own_acc[...] += adapter_scale * nn_dot(middle, up_full)
 
@@ -592,16 +597,16 @@
 
         out[rows, :] = own_acc[rows, :].astype(bf16)
 
-    for c in dn_sends + a_sends + g_sends + q_sends + kv_sends + mid_sends:
-        c.wait_send()
-
-    @pl.loop(0, n - 1)
-    def _(i):
-        d = dest(i)
-
-        @pl.loop(0, waves)
-        def _(wave):
-            hop(d, wave, jnp.where(d > t, 1, 0)).wait_send()
+    for part in range(2):
+        whole(dn_b.at[pl.ds(0, reps - 1), ranks[part]], dn_ssem.at[part]).wait()
+    for f in range(len(spread)):
+        whole(spread[f].at[pl.ds(0, half_reps - 1)], a_ssem.at[f]).wait()
+        whole(gathered[f].at[pl.ds(0, groups * (n - 1))], g_ssem.at[f]).wait()
+        whole(gathered[f].at[pl.ds(0, groups * n)], g_fsem.at[f]).wait()
+    shared(q_part, inner_r.at[0], in_ssem.at[0]).wait()
+    shared(kv_part, inner_r.at[1], in_ssem.at[1]).wait()
+    shared(mid_part, mid_r, mid_ssem).wait()
+    whole(rs_s.at[pl.ds(0, n - 1)], rs_ssem).wait()
 
 
 def local(
@@ -646,7 +651,7 @@
     pad_heads = -(-heads // 8) * 8
     wide = depth // n
     rows = seqs * pad_heads
-    steps, parts, waves = 16, 4, seqs // 16
+    steps, parts, waves = 8, 2, seqs // 16
     dma = pltpu.SemaphoreType.DMA
     hbm = pl.BlockSpec(memory_space=pl.ANY)
     vmem = pl.BlockSpec(memory_space=pltpu.VMEM)
@@ -654,7 +659,7 @@
     return pl.pallas_call(
         functools.partial(kernel, dims),
         name="decode_block",
-        out_shape=jax.ShapeDtypeStruct((seqs, wide), bf16),
+        out_shape=pltpu.VMEM((seqs, wide), bf16),
         in_specs=[hbm] * 13,
         out_specs=vmem,
         scratch_shapes=[
@@ -691,20 +696,20 @@
             dma((parts,)),
             dma((parts,)),
             dma((1 + len(factors),)),
-            dma((2, reps // 2)),
-            dma((2, reps)),
-            dma((2, reps // 2)),
-            dma((len(factors), reps // 2)),
-            dma((len(factors), reps // 2)),
-            dma((len(factors), reps)),
-            dma((len(factors), reps)),
-            dma((len(factors), reps)),
-            dma((2, n)),
-            dma((2, n)),
-            dma((n,)),
-            dma((n,)),
-            dma((n, waves)),
+            dma((2,)),
+            dma((2, 2)),
+            dma((len(factors),)),
+            dma((len(factors),)),
+            dma((len(factors),)),
+            dma((len(factors), 2)),
+            dma((len(factors),)),
+            dma((2,)),
+            dma((2,)),
+            dma,
+            dma,
+            dma,
             dma((n + 1, waves)),
+            pltpu.SemaphoreType.REGULAR((n - 2,)),
         ],
         compiler_params=pltpu.CompilerParams(
             collective_id=0, has_side_effects=True, vmem_limit_bytes=66000000

time: 44.5 us -> 39.2 us (0.88)
  the two profiles are of different devices: /device:TPU:0 before, /device:TPU:8 now
where the time goes in v2:
time: 39.2 us; the launch traced here: 39.1 us
  Pallas kernels  38.4 us (98%)
  local copies, waits for them, and re-layouts  0.71 us (2%)
    pallas_call x1, Pallas kernels, local(): pl.pallas_call(functools.partial(kernel, dims), name='decode_block', out_...  38.4 us

profile of v2, /device:TPU:8, one launch (start us, length us, event | category | flops | bytes accessed | tf_op | source)
XLA Modules:
  0.0 39.1 jit_solution(4849036729723276901)
XLA Ops:
  0.0 38.4 %decode_block.1 = bf16[64,2048]{1,0:T(8,128)(2,1)S(1)} custom-call(bf16[64,8192]{1,0:T(8,128)(2,1)} %hidden.1, bf16[8192]{0:T(1024)(128)(2,1)} %gain.1, bf16[8192,1024]{1,0:T(8,128)(2,1)} %wq.1, bf16[2,8192,256]{2,1,0:T(8,128)(2,1)} %wkv.1, bf16[1024,8192]{1,0:T(8,128)(2,1)} %wo.1, bf16[192,256]{1,0:T(8,128)(2,1)} %bitcast.5, bf16[64,128]{1,0:T(8,128)(2,1)} %f_q.1, ...), custom_call_target="tpu_custom_call" | custom-call | tf_op jit(solution)/shard_map/decode_block/pallas_call | solution.py:659
  38.4 0.7 %copy.15 = bf16[64,2048]{1,0:T(8,128)(2,1)} copy(bf16[64,2048]{1,0:T(8,128)(2,1)S(1)} %decode_block.1) | data formatting | bytes 524288

commit v3 on v2

--- a/solution.py
+++ b/solution.py
@@ -245,9 +245,15 @@
         here = dn_b.at[src, ranks[part]]
         return remote(here, here, dn_ssem.at[part], dn_rsem.at[part, way], rr, t)
 
+    def chip(j):
+        if half_reps != 4:
+            return lax.rem(mine_at + j, half_reps)
+        aside = mine_at + 1 - 2 * lax.rem(mine_at, 2)
+        return (half_reps - 1 - mine_at, aside, half_reps - 1 - aside)[j - 1]
+
     def send_down(part):
         for j in range(1, half_reps):
-            down(r, part, 0, lax.rem(partner + 2 * j, reps)).start()
+            down(r, part, 0, 2 * chip(j) + 1 - core).start()
         down(r, part, 1, partner).start()
 
     def relay_down(part):
@@ -301,7 +307,7 @@
         own_f[f].wait()
         for j in range(1, half_reps):
             remote(
-                here, here, a_ssem.at[f], a_rsem.at[f], lax.rem(r + 2 * j, reps), t
+                here, here, a_ssem.at[f], a_rsem.at[f], 2 * chip(j) + core, t
             ).start()
 
     per_plane = reps // n
@@ -321,9 +327,62 @@
             src = (t * per_plane + 2 * i) // 2
             pltpu.make_async_copy(buf.at[src], full.at[s], g_rsem.at[f, 0]).start()
 
+    home = r // per_plane
+    group_at = n * lax.rem(r, per_plane)
+    rooted = home == t
+
+    def to_root(f):
+        full = gathered[f]
+        here, there = spread[f].at[mine_at], full.at[group_at + t]
+        own_f[f].wait()
+
+        @pl.when(rooted)
+        def _():
+            pltpu.make_async_copy(here, there, g_rsem.at[f, 0]).start()
+
+        @pl.when(jnp.logical_not(rooted))
+        def _():
+            remote(here, there, g_ssem.at[f], g_rsem.at[f, 0], r, home).start()
+
+    def from_root(f):
+        mine = gathered[f].at[pl.ds(group_at, n)]
+
+        @pl.when(rooted)
+        def _():
+            whole(mine, g_rsem.at[f, 0]).wait()
+            for j in range(1, half_reps):
+                remote(
+                    mine, mine, a_ssem.at[f], a_rsem.at[f], lax.rem(r + 2 * j, reps), t
+                ).start()
+
+    def root_settled(f):
+        full = gathered[f]
+
+        @pl.when(rooted)
+        def _():
+            if groups > 1:
+                whole(full.at[pl.ds(0, (groups - 1) * n)], a_rsem.at[f]).wait()
+
+        @pl.when(jnp.logical_not(rooted))
+        def _():
+            whole(full.at[pl.ds(0, groups * n)], a_rsem.at[f]).wait()
+
+    def root_sent(f):
+        @pl.when(rooted)
+        def _():
+            for _j in range(1, half_reps):
+                whole(gathered[f].at[pl.ds(0, n)], a_ssem.at[f]).wait()
+
+        @pl.when(jnp.logical_not(rooted))
+        def _():
+            whole(gathered[f].at[0], g_ssem.at[f]).wait()
+
     def across(f):
         full = gathered[f]
-        whole(full.at[pl.ds(0, groups * n)], g_rsem.at[f, 0]).wait()
+        if f < 2:
+            whole(full.at[pl.ds(0, groups * n)], g_rsem.at[f, 0]).wait()
+        else:
+            root_settled(f)
         for i in range(groups):
             here = full.at[pl.ds(n * (2 * i + core), n)]
             remote(here, here, g_fsem.at[f], g_rsem.at[f, 1], partner, t).start()
@@ -331,13 +390,11 @@
     def settled(f):
         whole(gathered[f].at[pl.ds(0, groups * n)], g_rsem.at[f, 1]).wait()
 
-    to_chips(0)
     own_dn.wait()
-    send_down(0)
-    to_chips(1)
-    send_down(1)
-    to_chips(2)
-    to_chips(3)
+    for part in range(2):
+        pl.when(core == 0)(functools.partial(send_down, part))
+        to_chips(part)
+        pl.when(core == 1)(functools.partial(send_down, part))
 
     gain_in.wait()
     hid.wait()
@@ -370,19 +427,23 @@
         if k < n - 3:
             tell(k + 1)
 
-    project(0, 2)
+    project(0, 1)
     heard(0)
-    project(2, 2)
+    project(1, 2)
     for k in range(1, n - 2):
         heard(k)
+    project(3, 1)
     to_planes(0)
+    to_root(2)
+    to_root(3)
     project(4, 1)
     relay_down(0)
     project(5, 1)
     q_part = share_inner(0)
-    project(6, 2)
+    project(6, 1)
     to_planes(1)
     relay_down(1)
+    project(7, 1)
     len_in.wait()
 
     half_dim = head_dim // 2
@@ -504,11 +565,11 @@
                 pl.ds(wave * ws * pad_heads + h, ws, stride=pad_heads), :
             ].astype(bf16)
 
-    def hop(d, wave, up):
+    def hop(d, wave, up, cols=slice(None)):
         rows = pl.ds(pl.multiple_of(wave * ws, ws), ws)
         slot = d + up
         return remote(
-            rs_s.at[d, rows], rs_r.at[slot, rows], rs_ssem,
+            rs_s.at[d, rows, cols], rs_r.at[slot, rows, cols], rs_ssem,
             rs_rsem.at[slot, wave], r, t + 2 * up - 1,
         )
 
@@ -516,21 +577,24 @@
         d = dest(i)
         up = jnp.where(d > t, 1, 0)
         rows = pl.ds(pl.multiple_of(wave * ws, ws), ws)
+        fed = jnp.where(d > t, t > 0, t < n - 1)
         for j in range(wide // tile):
-            cols = slice(j * tile, (j + 1) * tile)
-            part_f[:, cols] = nn_dot(ctx[rows, :], wo_b[d, :, cols])
-        fed = jnp.where(d > t, t > 0, t < n - 1)
-
-        @pl.when(fed)
-        def _():
-            hop(d, wave, up).wait_recv()
-            rs_s[d, rows, :] = (part_f[...] + rs_r[d + up, rows, :].astype(f32)).astype(bf16)
-
-        @pl.when(jnp.logical_not(fed))
-        def _():
-            rs_s[d, rows, :] = part_f[...].astype(bf16)
-
-        hop(d, wave, up).start()
+            cols = pl.ds(j * tile, tile)
+            part_f[...] = nn_dot(ctx[rows, :], wo_b[d, :, cols])
+
+            @pl.when(fed)
+            def _():
+                if j == 0:
+                    hop(d, wave, up).wait_recv()
+                rs_s[d, rows, cols] = (
+                    part_f[...] + rs_r[d + up, rows, cols].astype(f32)
+                ).astype(bf16)
+
+            @pl.when(jnp.logical_not(fed))
+            def _():
+                rs_s[d, rows, cols] = part_f[...].astype(bf16)
+
+            hop(d, wave, up, cols).start()
 
     waves = rs_rsem.shape[1]
     ws = seqs // waves
@@ -538,8 +602,8 @@
     ahead = min(2, waves)
     pl.loop(0, blocks)(attend)
     across(1)
-    to_planes(2)
-    to_planes(3)
+    from_root(2)
+    from_root(3)
     pl.loop(blocks, ahead * blocks)(attend)
     settled(1)
     new_pair()
@@ -561,15 +625,22 @@
     mid_part = nt_dot(ctx[...], down_t)
     share(packed(mid_part), mid_s, mid_r, mid_ssem, mid_rsem)
 
-    @pl.loop(jnp.where(at_end, 1, 0), n - 1)
-    def _(i):
-        @pl.when(i > 0)
-        def _():
-            wo_copy(dest(i)).wait()
-
+    @pl.when(jnp.logical_not(at_end))
+    def _():
         @pl.loop(0, waves)
         def _(wave):
-            pass_on(i, wave)
+            pass_on(0, wave)
+
+    @pl.loop(0, (n - 2) * waves)
+    def _(s):
+        i = 1 + jnp.where(at_end, s // waves, s % (n - 2))
+        wave = jnp.where(at_end, s % waves, s // (n - 2))
+
+        @pl.when(wave == 0)
+        def _():
+            wo_copy(dest(i)).wait()
+
+        pass_on(i, wave)
 
     across(3)
     wo_copy(t).wait()
@@ -600,8 +671,11 @@
     for part in range(2):
         whole(dn_b.at[pl.ds(0, reps - 1), ranks[part]], dn_ssem.at[part]).wait()
     for f in range(len(spread)):
-        whole(spread[f].at[pl.ds(0, half_reps - 1)], a_ssem.at[f]).wait()
-        whole(gathered[f].at[pl.ds(0, groups * (n - 1))], g_ssem.at[f]).wait()
+        if f < 2:
+            whole(spread[f].at[pl.ds(0, half_reps - 1)], a_ssem.at[f]).wait()
+            whole(gathered[f].at[pl.ds(0, groups * (n - 1))], g_ssem.at[f]).wait()
+        else:
+            root_sent(f)
         whole(gathered[f].at[pl.ds(0, groups * n)], g_fsem.at[f]).wait()
     shared(q_part, inner_r.at[0], in_ssem.at[0]).wait()
     shared(kv_part, inner_r.at[1], in_ssem.at[1]).wait()
@@ -684,7 +758,7 @@
             vec((seqs, width), bf16),
             vec((seqs, 2 * rank), bf16),
             vec((n, seqs, 2 * rank), bf16),
-            vec((seqs // waves, wide), f32),
+            vec((seqs // waves, min(1024, wide)), f32),
             vec((seqs, wide), f32),
             vec((n, seqs, wide), bf16),
             vec((n + 1, seqs, wide), bf16),

time: 39.2 us -> 38.5 us (0.982)
  the two profiles are of different devices: /device:TPU:8 before, /device:TPU:0 now
where the time goes in v3:
time: 38.5 us; the launch traced here: 38.3 us
  Pallas kernels  37.6 us (98%)
  local copies, waits for them, and re-layouts  0.71 us (2%)
    pallas_call x1, Pallas kernels, local(): pl.pallas_call(functools.partial(kernel, dims), name='decode_block', out_...  37.6 us

profile of v3, /device:TPU:0, one launch (start us, length us, event | category | flops | bytes accessed | tf_op | source)
XLA Modules:
  0.0 38.3 jit_solution(6548654342483683736)
XLA Ops:
  0.0 37.6 %decode_block.1 = bf16[64,2048]{1,0:T(8,128)(2,1)S(1)} custom-call(bf16[64,8192]{1,0:T(8,128)(2,1)} %hidden.1, bf16[8192]{0:T(1024)(128)(2,1)} %gain.1, bf16[8192,1024]{1,0:T(8,128)(2,1)} %wq.1, bf16[2,8192,256]{2,1,0:T(8,128)(2,1)} %wkv.1, bf16[1024,8192]{1,0:T(8,128)(2,1)} %wo.1, bf16[192,256]{1,0:T(8,128)(2,1)} %bitcast.5, bf16[64,128]{1,0:T(8,128)(2,1)} %f_q.1, ...), custom_call_target="tpu_custom_call" | custom-call | tf_op jit(solution)/shard_map/decode_block/pallas_call | solution.py:733
  37.6 0.7 %copy.15 = bf16[64,2048]{1,0:T(8,128)(2,1)} copy(bf16[64,2048]{1,0:T(8,128)(2,1)S(1)} %decode_block.1) | data formatting | bytes 524288

commit v4 on v3

--- a/solution.py
+++ b/solution.py
@@ -262,12 +262,18 @@
             down(lax.rem(partner + 2 * j, reps), part, 1, partner).start()
 
     def share_inner(part):
+        def some(first):
+            total = jnp.zeros((seqs, (1 + part) * rank), f32)
+            for k in range(half_reps):
+                j = first if k == 0 else lax.rem(r + partner - first + 2 * k, reps)
+                start = (j * n + t) * block
+                cols = pl.ds(pl.multiple_of(start // win * win, LANES), win)
+                total = total + nt_dot(norm_b[:, cols], dn_b[j, ranks[part]])
+            return total
+
+        total = some(r)
         whole(dn_b.at[pl.ds(0, half_reps), ranks[part]], dn_rsem.at[part, 1]).wait()
-        total = jnp.zeros((seqs, (1 + part) * rank), f32)
-        for j in range(reps):
-            start = (j * n + t) * block
-            cols = pl.ds(pl.multiple_of(start // win * win, LANES), win)
-            total = total + nt_dot(norm_b[:, cols], dn_b[j, ranks[part]])
+        total = total + some(partner)
         share(packed(total), inner_s.at[part], inner_r.at[part], in_ssem.at[part], in_rsem.at[part])
         return total
 
@@ -391,10 +397,11 @@
         whole(gathered[f].at[pl.ds(0, groups * n)], g_rsem.at[f, 1]).wait()
 
     own_dn.wait()
-    for part in range(2):
-        pl.when(core == 0)(functools.partial(send_down, part))
-        to_chips(part)
-        pl.when(core == 1)(functools.partial(send_down, part))
+    pl.when(core == 0)(functools.partial(send_down, 0))
+    to_chips(0)
+    pl.when(core == 1)(functools.partial(send_down, 0))
+    send_down(1)
+    to_chips(1)
 
     gain_in.wait()
     hid.wait()

time: 38.5 us -> 38.3 us (level)
  no operation moved by 1% of the time
where the time goes in v4:
time: 38.3 us; the launch traced here: 38.1 us
  Pallas kernels  37.4 us (98%)
  local copies, waits for them, and re-layouts  0.71 us (2%)
    pallas_call x1, Pallas kernels, local(): pl.pallas_call(functools.partial(kernel, dims), name='decode_block', out_...  37.4 us

profile of v4, /device:TPU:0, one launch (start us, length us, event | category | flops | bytes accessed | tf_op | source)
XLA Modules:
  0.0 38.1 jit_solution(7337324366336761532)
XLA Ops:
  0.0 37.4 %decode_block.1 = bf16[64,2048]{1,0:T(8,128)(2,1)S(1)} custom-call(bf16[64,8192]{1,0:T(8,128)(2,1)} %hidden.1, bf16[8192]{0:T(1024)(128)(2,1)} %gain.1, bf16[8192,1024]{1,0:T(8,128)(2,1)} %wq.1, bf16[2,8192,256]{2,1,0:T(8,128)(2,1)} %wkv.1, bf16[1024,8192]{1,0:T(8,128)(2,1)} %wo.1, bf16[192,256]{1,0:T(8,128)(2,1)} %bitcast.5, bf16[64,128]{1,0:T(8,128)(2,1)} %f_q.1, ...), custom_call_target="tpu_custom_call" | custom-call | tf_op jit(solution)/shard_map/decode_block/pallas_call | solution.py:740
  37.4 0.7 %copy.15 = bf16[64,2048]{1,0:T(8,128)(2,1)} copy(bf16[64,2048]{1,0:T(8,128)(2,1)S(1)} %decode_block.1) | data formatting | bytes 524288
